TPU v7x, 32 devices: a whole 2x2x4 slice. The times are simulated.
32 devices in a mesh: dp: 4 (over y, core), tensor: 8 (over z, x).
Axes of the slice: x: 2, y: 2, z: 4, core: 2. Of those that a mesh axis runs over, the one named last changes fastest.
Arguments:
- ref_hidden: bfloat16 [1152, 4608], P('dp', 'tensor'), may hold values from -6 to 6
- pol_hidden: bfloat16 [1152, 4608], P('dp', 'tensor'), may hold values from -6 to 6
- readout: bfloat16 [1152, 4608], P('dp', 'tensor'), may hold values from -0.019897461 to 0.019897461
- lengths: int32 [12], P('dp'), may hold values from 16 to 96, as said below
- pairing: int32 [12], replicated, may hold values from 0 to 11, each once
- pre_gain: float32 [4608], replicated, may hold values from 0.25 to 1.75
- post_gain: float32 [4608], replicated, may hold values from 0.25 to 1.75
- w_query: bfloat16 [4608, 4096], P('dp', 'tensor'), may hold values from -0.09375 to 0.09375
- w_key: bfloat16 [4608, 2048], P('dp', 'tensor'), may hold values from -3 to 3
- value_projection: bfloat16 [4608, 2048], P('dp', 'tensor'), may hold values from -0.09375 to 0.09375
- w_out: bfloat16 [4608, 4096], P('dp', 'tensor'), may hold values from -0.09375 to 0.09375
- a_query: bfloat16 [4608, 64], P('dp'), may hold values from -0.09375 to 0.09375
- a_value: bfloat16 [4608, 64], P('dp'), may hold values from -0.09375 to 0.09375
- query_second_factor: bfloat16 [64, 4096], P(None, 'tensor'), may hold values from -0.75 to 0.75
- value_second_factor: bfloat16 [64, 2048], P(None, 'tensor'), may hold values from -0.75 to 0.75
Outputs:
- policy_out: bfloat16 [1152, 4608], P('dp', 'tensor')
- reference_out: bfloat16 [1152, 4608], P('dp', 'tensor')
- dpo_loss: float32 [], replicated
- grad_hidden: bfloat16 [1152, 4608], P('dp', 'tensor')
- grad_a: float32 [4608, 128], P('dp')
- query_factor_gradient: float32 [64, 4096], P(None, 'tensor')
- value_factor_gradient: float32 [64, 2048], P(None, 'tensor')
Inputs may be any that keep to these rules, and one draw needn't show every extreme that they name: `lengths`: every sequence has at least one valid token and some sequence is full. `pairing`: entries 2k and 2k + 1 name the chosen and the rejected sequence of pair k; every sequence appears once.
All inputs are finite; a program needn't handle non-finite values.
Results may differ from a plain program's by a relative error of at most 0.0233.
The roundings to bfloat16 on the way count: a program that leaves them out, or rounds other values in their place, can miss the bound.
Values may be sent and summed in bfloat16 or wider, within the bound.
A program may use at most 128 MiB of HBM per device.

v0:
```python
import jax
import jax.numpy as jnp
from jax import lax
from jax.sharding import PartitionSpec as P

MODEL_WIDTH = 4608
HQ = 32
HEAD_SIZE = 128
NORM_EPS = 1e-06
SOFT_CAP = 50.0
ADAPTER_SCALE = 0.5
DPO_BETA = 0.5
LOSS_SCALE = 256.0
ROPE_BASE = 10000.0


def query_scale():
    return float(MODEL_WIDTH // HQ) ** (-0.5)


def apply_rotation(value_rows, direction):
    length = value_rows.shape[1]
    head_depth = value_rows.shape[3]
    middle = head_depth // 2
    spacing = ROPE_BASE ** (-2.0 * jnp.arange(middle, dtype=jnp.float32) / head_depth)
    angles = jnp.arange(length, dtype=jnp.float32)[:, None] * spacing[None, :]
    cosine = jnp.cos(angles)[None, :, None, :]
    sine_part = direction * jnp.sin(angles)[None, :, None, :]
    leading = value_rows[..., :middle]
    trailing = value_rows[..., middle:]
    return jnp.concatenate(
        [leading * cosine - trailing * sine_part, trailing * cosine + leading * sine_part], axis=-1
    )


def allowed_mask(lengths, length):
    places = jnp.arange(length)
    causal = places[None, :] <= places[:, None]
    living = places[None, :] < lengths[:, None]
    return causal[None, None, None, :, :] & living[:, None, None, None, :]


def attend(query_rows, rotated_keys, value_rows, lengths):
    seqs_here, length, q_heads, head_depth = query_rows.shape
    kv_heads = rotated_keys.shape[2]
    grouped_heads = query_rows.reshape(seqs_here, length, kv_heads, q_heads // kv_heads, head_depth)
    scores = (
        jnp.einsum(
            "sqkgd,spkd->skgqp", grouped_heads, rotated_keys, preferred_element_type=jnp.float32
        )
        * query_scale()
    )
    capped = SOFT_CAP * jnp.tanh(scores / SOFT_CAP)
    allowed = allowed_mask(lengths, length)
    weights = jnp.where(allowed, jnp.exp(capped), 0.0)
    probabilities = weights / jnp.sum(weights, axis=-1, keepdims=True)
    probs_low = probabilities.astype(jnp.bfloat16)
    mixed_out = jnp.einsum(
        "skgqp,spkd->sqkgd", probs_low, value_rows, preferred_element_type=jnp.float32
    )
    return (
        mixed_out.astype(jnp.bfloat16).reshape(seqs_here, length, q_heads, head_depth),
        probs_low,
        probabilities,
        capped,
    )


def attend_back(grad_mixed, query_rows, rotated_keys, value_rows, probs_low, probabilities, capped):
    seqs_here, length, q_heads, head_depth = query_rows.shape
    kv_heads = rotated_keys.shape[2]
    shape_five = (seqs_here, length, kv_heads, q_heads // kv_heads, head_depth)
    grouped_heads = query_rows.reshape(shape_five)
    grad_grouped = grad_mixed.reshape(shape_five)
    grad_probs = jnp.einsum(
        "sqkgd,spkd->skgqp", grad_grouped, value_rows, preferred_element_type=jnp.float32
    )
    value_rows_gradient = jnp.einsum(
        "skgqp,sqkgd->spkd", probs_low, grad_grouped, preferred_element_type=jnp.float32
    )
    centered = grad_probs - jnp.sum(grad_probs * probabilities, axis=-1, keepdims=True)
    grad_scores = (
        probabilities * centered * (1.0 - (capped / SOFT_CAP) ** 2) * query_scale()
    ).astype(jnp.bfloat16)
    query_rows_gradient = jnp.einsum(
        "skgqp,spkd->sqkgd", grad_scores, rotated_keys, preferred_element_type=jnp.float32
    ).reshape(seqs_here, length, q_heads, head_depth)
    key_rows_gradient = jnp.einsum(
        "skgqp,sqkgd->spkd", grad_scores, grouped_heads, preferred_element_type=jnp.float32
    )
    return (query_rows_gradient, key_rows_gradient, value_rows_gradient)


def normalize(hidden, pre_gain):
    whole_rows = lax.all_gather(hidden, "tensor", axis=1, tiled=True)
    wide_rows = whole_rows.astype(jnp.float32)
    pre_scale = lax.rsqrt(
        jnp.sum(wide_rows * wide_rows, axis=1, keepdims=True) / pre_gain.shape[0] + NORM_EPS
    )
    normed = (wide_rows * pre_scale * pre_gain).astype(jnp.bfloat16)
    return (normed, pre_scale)


def attention_layer(hidden, normed, weights, adapters, lengths, post_local):
    w_query, w_key, value_projection, w_out, a_query, a_value = weights
    tok_rows, full_width = normed.shape
    seqs_here = lengths.shape[0]
    length = tok_rows // seqs_here
    query_rows = jnp.dot(normed, w_query, preferred_element_type=jnp.float32)
    keys_before_rotation = jnp.dot(normed, w_key, preferred_element_type=jnp.float32)
    value_rows = jnp.dot(normed, value_projection, preferred_element_type=jnp.float32)
    low_rank_update = None
    if adapters is not None:
        query_second_factor, value_second_factor = adapters
        rank_size = query_second_factor.shape[0]
        low_rank_update = jnp.dot(
            normed, jnp.concatenate([a_query, a_value], axis=1), preferred_element_type=jnp.float32
        ).astype(jnp.bfloat16)
        query_rows = query_rows + ADAPTER_SCALE * jnp.dot(
            low_rank_update[:, :rank_size], query_second_factor, preferred_element_type=jnp.float32
        )
        value_rows = value_rows + ADAPTER_SCALE * jnp.dot(
            low_rank_update[:, rank_size:], value_second_factor, preferred_element_type=jnp.float32
        )
    q_heads = query_rows.shape[1] // HEAD_SIZE
    kv_heads = keys_before_rotation.shape[1] // HEAD_SIZE
    query_rows = apply_rotation(
        query_rows.reshape(seqs_here, length, q_heads, HEAD_SIZE), 1.0
    ).astype(jnp.bfloat16)
    rotated_keys = apply_rotation(
        keys_before_rotation.reshape(seqs_here, length, kv_heads, HEAD_SIZE), 1.0
    ).astype(jnp.bfloat16)
    value_rows = value_rows.reshape(seqs_here, length, kv_heads, HEAD_SIZE).astype(jnp.bfloat16)
    mixed_out, probs_low, probabilities, capped = attend(
        query_rows, rotated_keys, value_rows, lengths
    )
    head_terms = lax.dot_general(
        mixed_out.reshape(tok_rows, q_heads * HEAD_SIZE),
        w_out,
        (((1,), (1,)), ((), ())),
        preferred_element_type=jnp.float32,
    )
    summed = lax.psum_scatter(
        head_terms.astype(jnp.bfloat16), "tensor", scatter_dimension=1, tiled=True
    ).astype(jnp.float32)
    squares = lax.psum(jnp.sum(summed * summed, axis=1), "tensor")
    post_scale = lax.rsqrt(squares[:, None] / full_width + NORM_EPS)
    result = hidden.astype(jnp.float32) + summed * post_scale * post_local
    saved = (
        low_rank_update,
        query_rows,
        rotated_keys,
        value_rows,
        probs_low,
        probabilities,
        capped,
        summed,
        post_scale,
    )
    return (result, saved)


def body(
    ref_hidden,
    pol_hidden,
    readout,
    lengths,
    pairing,
    pre_gain,
    post_gain,
    w_query,
    w_key,
    value_projection,
    w_out,
    a_query,
    a_value,
    query_second_factor,
    value_second_factor,
):
    tok_rows, part_width = pol_hidden.shape
    seqs_here = lengths.shape[0]
    length = tok_rows // seqs_here
    tensor_rank = lax.axis_index("tensor")
    data_rank = lax.axis_index("dp")
    all_seqs = seqs_here * lax.axis_size("dp")
    full_width = part_width * lax.axis_size("tensor")
    pre_local = lax.dynamic_slice_in_dim(pre_gain, tensor_rank * part_width, part_width)
    post_local = lax.dynamic_slice_in_dim(post_gain, tensor_rank * part_width, part_width)
    weights = (
        lax.all_gather(w_query, "dp", axis=0, tiled=True),
        lax.all_gather(w_key, "dp", axis=0, tiled=True),
        lax.all_gather(value_projection, "dp", axis=0, tiled=True),
        lax.all_gather(w_out, "dp", axis=0, tiled=True),
        lax.all_gather(a_query, "dp", axis=0, tiled=True),
        lax.all_gather(a_value, "dp", axis=0, tiled=True),
    )
    w_query_all, w_key_all, w_value_all, w_out_all, a_query_all, a_value_all = weights
    ref_normed, ref_scale = normalize(ref_hidden, pre_gain)
    ref_result, ref_saved = attention_layer(
        ref_hidden, ref_normed, weights, None, lengths, post_local
    )
    pol_normed, pol_scale = normalize(pol_hidden, pre_gain)
    pol_result, pol_saved = attention_layer(
        pol_hidden,
        pol_normed,
        weights,
        (query_second_factor, value_second_factor),
        lengths,
        post_local,
    )
    readout_wide = readout.astype(jnp.float32)
    living = (jnp.arange(length)[None, :] < lengths[:, None]).astype(jnp.float32)

    def sequence_score(result):
        return jnp.sum(
            jnp.sum(result * readout_wide, axis=1).reshape(seqs_here, length) * living, axis=1
        )

    placed = jnp.zeros((2, all_seqs), jnp.float32)
    offset = data_rank * seqs_here
    placed = lax.dynamic_update_slice(
        placed,
        jnp.stack([sequence_score(ref_result), sequence_score(pol_result)]),
        (jnp.int32(0), offset),
    )
    scores = lax.psum(placed, ("dp", "tensor"))
    ratios = scores[1] - scores[0]
    chooser = (pairing[:, None] == jnp.arange(all_seqs)[None, :]).astype(jnp.float32)
    picked = jnp.dot(chooser, ratios, precision=lax.Precision.HIGHEST).reshape(-1, 2)
    margins = DPO_BETA * (picked[:, 0] - picked[:, 1])
    dpo_loss = jnp.sum(jax.nn.softplus(-margins))
    pair_pull = DPO_BETA * LOSS_SCALE * jax.nn.sigmoid(-margins)
    signed = jnp.stack([-pair_pull, pair_pull], axis=1).reshape(-1)
    coefficients = jnp.dot(signed, chooser, precision=lax.Precision.HIGHEST)
    local_coef = lax.dynamic_slice_in_dim(coefficients, offset, seqs_here)
    grad_result = (local_coef[:, None] * living).reshape(tok_rows, 1) * readout_wide
    (
        low_rank_update,
        query_rows,
        rotated_keys,
        value_rows,
        probs_low,
        probabilities,
        capped,
        summed,
        post_scale,
    ) = pol_saved
    post_dot = lax.psum(jnp.sum(summed * post_local * grad_result, axis=1), "tensor")
    grad_summed = (
        post_scale * post_local * grad_result
        - summed * post_scale**3 * post_dot[:, None] / full_width
    )
    grad_wide = lax.all_gather(grad_summed.astype(jnp.bfloat16), "tensor", axis=1, tiled=True)
    grad_mixed = jnp.dot(grad_wide, w_out_all, preferred_element_type=jnp.float32).astype(
        jnp.bfloat16
    )
    q_heads = query_rows.shape[2]
    grad_q_rot, rotated_key_gradient, value_head_gradient = attend_back(
        grad_mixed.reshape(seqs_here, length, q_heads, HEAD_SIZE),
        query_rows,
        rotated_keys,
        value_rows,
        probs_low,
        probabilities,
        capped,
    )
    query_rows_gradient = (
        apply_rotation(grad_q_rot, -1.0).reshape(tok_rows, -1).astype(jnp.bfloat16)
    )
    key_rows_gradient = (
        apply_rotation(rotated_key_gradient, -1.0).reshape(tok_rows, -1).astype(jnp.bfloat16)
    )
    value_rows_gradient = value_head_gradient.reshape(tok_rows, -1).astype(jnp.bfloat16)
    rank_size = query_second_factor.shape[0]
    rows_contraction = (((0,), (0,)), ((), ()))
    contract_cols = (((1,), (1,)), ((), ()))
    query_adapter_term = ADAPTER_SCALE * lax.dot_general(
        low_rank_update[:, :rank_size],
        query_rows_gradient,
        rows_contraction,
        preferred_element_type=jnp.float32,
    )
    value_adapter_term = ADAPTER_SCALE * lax.dot_general(
        low_rank_update[:, rank_size:],
        value_rows_gradient,
        rows_contraction,
        preferred_element_type=jnp.float32,
    )
    query_factor_gradient, value_factor_gradient = (
        lax.psum(query_adapter_term.astype(jnp.bfloat16), "dp").astype(jnp.float32),
        lax.psum(value_adapter_term.astype(jnp.bfloat16), "dp").astype(jnp.float32),
    )
    adapter_grad = jnp.concatenate(
        [
            ADAPTER_SCALE
            * lax.dot_general(
                query_rows_gradient,
                query_second_factor,
                contract_cols,
                preferred_element_type=jnp.float32,
            ),
            ADAPTER_SCALE
            * lax.dot_general(
                value_rows_gradient,
                value_second_factor,
                contract_cols,
                preferred_element_type=jnp.float32,
            ),
        ],
        axis=1,
    ).astype(jnp.bfloat16)
    adapter_term = lax.dot_general(
        pol_normed, adapter_grad, rows_contraction, preferred_element_type=jnp.float32
    )
    adapter_part = lax.psum_scatter(
        adapter_term.astype(jnp.bfloat16), "dp", scatter_dimension=0, tiled=True
    )
    grad_a = lax.psum(adapter_part, "tensor").astype(jnp.float32)
    a_both = jnp.concatenate([a_query_all, a_value_all], axis=1)
    input_terms = lax.dot_general(
        query_rows_gradient, w_query_all, contract_cols, preferred_element_type=jnp.float32
    )
    input_terms = input_terms + lax.dot_general(
        key_rows_gradient, w_key_all, contract_cols, preferred_element_type=jnp.float32
    )
    input_terms = input_terms + lax.dot_general(
        value_rows_gradient, w_value_all, contract_cols, preferred_element_type=jnp.float32
    )
    input_terms = input_terms + lax.dot_general(
        adapter_grad, a_both, contract_cols, preferred_element_type=jnp.float32
    )
    input_whole = lax.psum(input_terms.astype(jnp.bfloat16), "tensor").astype(jnp.float32)
    grad_normed = lax.dynamic_slice_in_dim(input_whole, tensor_rank * part_width, part_width, 1)
    narrow = pol_hidden.astype(jnp.float32)
    pre_dot = lax.psum(jnp.sum(narrow * pre_local * grad_normed, axis=1), "tensor")
    grad_hidden = (
        grad_result
        + pol_scale * pre_local * grad_normed
        - narrow * pol_scale**3 * pre_dot[:, None] / full_width
    )
    return (
        pol_result.astype(jnp.bfloat16),
        ref_result.astype(jnp.bfloat16),
        dpo_loss,
        grad_hidden.astype(jnp.bfloat16),
        grad_a,
        query_factor_gradient,
        value_factor_gradient,
    )


def solution(mesh):
    placed = (
        P("dp", "tensor"),
        P("dp", "tensor"),
        P("dp", "tensor"),
        P("dp"),
        P(),
        P(),
        P(),
        P("dp", "tensor"),
        P("dp", "tensor"),
        P("dp", "tensor"),
        P("dp", "tensor"),
        P("dp", None),
        P("dp", None),
        P(None, "tensor"),
        P(None, "tensor"),
    )
    return jax.shard_map(
        body,
        mesh=mesh,
        in_specs=placed,
        out_specs=(
            P("dp", "tensor"),
            P("dp", "tensor"),
            P(),
            P("dp", "tensor"),
            P("dp", None),
            P(None, "tensor"),
            P(None, "tensor"),
        ),
        check_vma=False,
    )
```

profile of v0, /device:TPU:0, one launch (start us, length us, event | category | flops | bytes accessed | tf_op | source)
XLA Modules:
  0.0 823.5 jit_solution(8016594998505936199)
XLA Ops:
  11.2 9.0 %all_gather.29 = bf16[4608,64]{0,1:T(8,128)(2,1)S(1)} all-gather(bf16[1152,64]{0,1:T(8,128)(2,1)S(1)} %copy-done.29), channel_id=1, replica_groups=mesh['dp'=4,'tensor'=8] {'dp'}, dimensions={0}, use_global_device_ids=true | all-gather | bytes 737280 | tf_op jit(solution)/shard_map/all_gather | solution.py:194
  20.3 7.6 all_gather.30
  29.8 41.2 %all-gather.21.cloned.1.call-done = bf16[8,576,288]{1,2,0:T(8,128)(2,1)} async-done(((bf16[1,576,288]{1,2,0:T(8,128)(2,1)}), bf16[8,576,288]{1,2,0:T(8,128)(2,1)}) %all-gather.21.cloned.1.call-update) | async-done | bytes 2654224 | tf_op jit(solution)/shard_map/all_gather | solution.py:95
  76.4 7.2 reshape.270
  83.6 46.3 %all-gather.19.cloned.1.call-done = bf16[8,576,288]{1,2,0:T(8,128)(2,1)} async-done(((bf16[1,576,288]{1,2,0:T(8,128)(2,1)}), bf16[8,576,288]{1,2,0:T(8,128)(2,1)}) %all-gather.19.cloned.1.call-update) | async-done | bytes 2654224 | tf_op jit(solution)/shard_map/all_gather | solution.py:95
  135.2 7.8 reshape.269
  162.0 17.6 %all-gather.11.cloned.1.call-done = bf16[4608,256]{1,0:T(8,128)(2,1)} async-done(((bf16[1152,256]{1,0:T(8,128)(2,1)}), bf16[4608,256]{1,0:T(8,128)(2,1)}) %all-gather.11.cloned.1.call-update) | async-done | bytes 2359312 | tf_op jit(solution)/shard_map/all_gather | solution.py:192
  186.1 32.4 %all-gather.15.cloned.1.call-done = bf16[4608,512]{1,0:T(8,128)(2,1)} async-done(((bf16[1152,512]{1,0:T(8,128)(2,1)}), bf16[4608,512]{1,0:T(8,128)(2,1)}) %all-gather.15.cloned.1.call-update) | async-done | bytes 4718608 | tf_op jit(solution)/shard_map/all_gather | solution.py:190
  218.5 5.5 fusion.142
  239.0 18.4 %all-gather.17.cloned.1.call-done = bf16[4608,512]{1,0:T(8,128)(2,1)} async-done(((bf16[1152,512]{1,0:T(8,128)(2,1)}), bf16[4608,512]{1,0:T(8,128)(2,1)}) %all-gather.17.cloned.1.call-update) | async-done | bytes 4718608 | tf_op jit(solution)/shard_map/all_gather | solution.py:193
  257.4 5.4 convolution_convert_fusion
  276.2 5.6 convolution_convert_fusion.1
  288.0 59.2 %reduce-scatter.12.cloned.1.call-done = bf16[576,288]{1,0:T(8,128)(2,1)} async-done(((bf16[4608,288]{1,0:T(8,128)(2,1)}), bf16[576,288]{1,0:T(8,128)(2,1)}) %reduce-scatter.12.cloned.1.call-update) | async-done | bytes 331792
  349.1 80.8 %reduce-scatter.10.cloned.1.call-done = bf16[576,288]{1,0:T(8,128)(2,1)} async-done(((bf16[4608,288]{1,0:T(8,128)(2,1)}), bf16[576,288]{1,0:T(8,128)(2,1)}) %reduce-scatter.10.cloned.1.call-update) | async-done | bytes 331792
  432.4 20.1 %all-reduce = (f32[288]{0:T(512)S(1)}, f32[288]{0:T(512)S(1)}) all-reduce(f32[288]{0:T(512)S(1)} %fusion.45, f32[288]{0:T(512)S(1)} %fusion.32), channel_id=1, replica_groups=mesh['dp'=4,'tensor'=8] {'tensor'}, use_global_device_ids=true, to_apply=%region_4.5 | all-reduce | flops 576 | bytes 4608 | tf_op jit(solution)/shard_map/psum | solution.py:146
  457.0 36.8 %psum.65 = f32[2,12]{1,0:T(2,128)S(1)} all-reduce(f32[2,12]{1,0:T(2,128)S(1)} %dynamic_update_slice.3), channel_id=1, replica_groups=mesh['dp'=4,'tensor'=8] {'dp','tensor'}, use_global_device_ids=true, to_apply=%region_14.15 | all-reduce | flops 24 | bytes 192 | tf_op jit(solution)/shard_map/psum | solution.py:226
  496.8 21.1 %psum.66 = f32[288]{0:T(512)S(1)} all-reduce(f32[288]{0:T(512)S(1)} %fusion.38), channel_id=1, replica_groups=mesh['dp'=4,'tensor'=8] {'tensor'}, use_global_device_ids=true, to_apply=%region_17.18 | all-reduce | flops 288 | bytes 2304 | tf_op jit(solution)/shard_map/psum | solution.py:248
  519.2 55.1 %all-gather.23.cloned.1.call-done = bf16[8,576,288]{1,2,0:T(8,128)(2,1)} async-done(((bf16[1,576,288]{1,2,0:T(8,128)(2,1)}), bf16[8,576,288]{1,2,0:T(8,128)(2,1)}) %all-gather.23.cloned.1.call-update) | async-done | bytes 2654224 | tf_op jit(solution)/shard_map/all_gather | solution.py:253
  578.8 5.6 reshape.268
  618.7 10.8 %reduce-scatter.8.cloned.1.call-done = bf16[1152,128]{1,0:T(8,128)(2,1)} async-done(((bf16[4608,128]{1,0:T(8,128)(2,1)}), bf16[1152,128]{1,0:T(8,128)(2,1)}) %reduce-scatter.8.cloned.1.call-update) | async-done | bytes 294928 | tf_op jit(solution)/shard_map/reduce_scatter | solution.py:315
  631.2 10.5 %psum.71 = bf16[64,256]{1,0:T(8,128)(2,1)S(1)} all-reduce(bf16[64,256]{1,0:T(8,128)(2,1)S(1)} %fusion.23), channel_id=1, replica_groups=mesh['dp'=4,'tensor'=8] {'dp'}, use_global_device_ids=true, to_apply=%region_25.26 | all-reduce | flops 16384 | bytes 65536 | tf_op jit(solution)/shard_map/psum | solution.py:291
  642.4 21.6 %all-reduce.5.cloned.1.call-done = bf16[64,512]{1,0:T(8,128)(2,1)} async-done(((bf16[64,512]{1,0:T(8,128)(2,1)}), bf16[64,512]{1,0:T(8,128)(2,1)}) %all-reduce.5.cloned.1.call-update) | async-done | bytes 65552 | tf_op jit(solution)/shard_map/psum | solution.py:290
  665.5 126.0 %all-reduce.7.cloned.1.call-done = (bf16[288,4608]{1,0:T(8,128)(2,1)}, bf16[1152,128]{1,0:T(8,128)(2,1)}) async-done(((bf16[288,4608]{1,0:T(8,128)(2,1)}, bf16[1152,128]{1,0:T(8,128)(2,1)}), (bf16[288,4608]{1,0:T(8,128)(2,1)}, bf16[1152,128]{1,0:T(8,128)(2,1)})) %all-reduce.7.cloned.1.call-update) | async-done | bytes 2949136 | tf_op jit(solution)/shard_map/psum | solution.py:332
  792.8 19.4 %psum.68 = f32[288]{0:T(512)S(1)} all-reduce(f32[288]{0:T(512)S(1)} %fusion.35), channel_id=1, replica_groups=mesh['dp'=4,'tensor'=8] {'tensor'}, use_global_device_ids=true, to_apply=%region_21.22 | all-reduce | flops 288 | bytes 2304 | tf_op jit(solution)/shard_map/psum | solution.py:335
  (219 shorter events, 137.3 us)
Async XLA Ops:
  7.2 222.5 %copy-start = (bf16[64,512]{1,0:T(8,128)(2,1)S(1)}, bf16[64,512]{1,0:T(8,128)(2,1)}, u32[]{:S(2)}) copy-start(bf16[64,512]{1,0:T(8,128)(2,1)} %param.28) | copy-start | bytes 196612
  7.2 63.8 %all-gather.21.cloned.1.call-start = ((), (), s32[]{:S(2)}) async-start(), calls=%async_computation.10 | async-start | bytes 3317760 | tf_op jit(solution)/shard_map/all_gather | solution.py:95
  7.9 121.9 %all-gather.19.cloned.1.call-start = ((), (), s32[]{:S(2)}) async-start(), calls=%async_computation.9 | async-start | bytes 3317760 | tf_op jit(solution)/shard_map/all_gather | solution.py:95
  8.7 11.6 %copy-start.30 = (bf16[1152,64]{0,1:T(8,128)(2,1)S(1)}, bf16[1152,64]{0,1:T(8,128)(2,1)}, u32[]{:S(2)}) copy-start(bf16[1152,64]{0,1:T(8,128)(2,1)} %param.27) | copy-start | bytes 442372
  8.7 145.4 %all-gather.13.cloned.1.call-start = ((), (), s32[]{:S(2)}) async-start(), calls=%async_computation.4 | async-start | bytes 2949120 | tf_op jit(solution)/shard_map/all_gather | solution.py:191
  9.4 170.2 %all-gather.11.cloned.1.call-start = ((), (), s32[]{:S(2)}) async-start(), calls=%async_computation.3 | async-start | bytes 2949120 | tf_op jit(solution)/shard_map/all_gather | solution.py:192
  10.0 18.0 %copy-start.40 = (s32[3]{0:T(128)S(1)}, s32[3]{0:T(128)}, u32[]{:S(2)}) copy-start(s32[3]{0:T(128)} %param.18) | copy-start | bytes 40
  10.0 208.5 %all-gather.15.cloned.1.call-start = ((), (), s32[]{:S(2)}) async-start(), calls=%async_computation.5 | async-start | bytes 5898240 | tf_op jit(solution)/shard_map/all_gather | solution.py:190
  10.6 246.8 %all-gather.17.cloned.1.call-start = ((), (), s32[]{:S(2)}) async-start(), calls=%async_computation.6 | async-start | bytes 5898240 | tf_op jit(solution)/shard_map/all_gather | solution.py:193
  11.2 336.0 %reduce-scatter.12.cloned.1.call-start = ((), (), s32[]{:S(2)}) async-start(), calls=%async_computation.13 | async-start | bytes 3981312
  28.1 48.3 %copy-start.3 = (bf16[4608,128]{0,1:T(8,128)(2,1)}, bf16[4608,128]{0,1:T(8,128)(2,1)S(1)}, u32[]{:S(2)}) copy-start(bf16[4608,128]{0,1:T(8,128)(2,1)S(1)} %constant_dynamic-update-slice_fusion) | copy-start | bytes 3538948
  29.8 203.0 %copy-start.12 = (f32[96,64]{1,0:T(8,128)}, f32[96,64]{1,0:T(8,128)S(1)}, u32[]{:S(2)}) copy-start(f32[96,64]{1,0:T(8,128)S(1)} %get-tuple-element.50) | copy-start | bytes 73732
  135.2 12.9 %copy-start.36 = (f32[4608]{0:T(1024)S(1)}, f32[4608]{0:T(1024)}, u32[]{:S(2)}) copy-start(f32[4608]{0:T(1024)} %param.20) | copy-start | bytes 55300
  267.6 162.2 %reduce-scatter.10.cloned.1.call-start = ((), (), s32[]{:S(2)}) async-start(), calls=%async_computation.12 | async-start | bytes 3981312
  286.5 166.0 %copy-start.6 = (bf16[288,576]{1,0:T(8,128)(2,1)S(1)}, bf16[288,576]{1,0:T(8,128)(2,1)}, u32[]{:S(2)}) copy-start(bf16[288,576]{1,0:T(8,128)(2,1)} %param.17) | copy-start | bytes 995332
  286.5 287.9 %all-gather.23.cloned.1.call-start = ((), (), s32[]{:S(2)}) async-start(), calls=%async_computation.11 | async-start | bytes 3317760 | tf_op jit(solution)/shard_map/all_gather | solution.py:253
  519.0 110.6 %reduce-scatter.8.cloned.1.call-start = ((), (), s32[]{:S(2)}) async-start(), calls=%async_computation.7 | async-start | bytes 1474560 | tf_op jit(solution)/shard_map/reduce_scatter | solution.py:315
  584.4 8.5 %copy-start.45 = (f32[3,2,2,96]{3,2,1,0:T(2,128)S(1)}, f32[3,2,2,96]{3,2,1,0:T(2,128)}, u32[]{:S(2)}) copy-start(f32[3,2,2,96]{3,2,1,0:T(2,128)} %copy-done.44) | copy-start | bytes 13828
  605.1 58.9 %all-reduce.5.cloned.1.call-start = ((), (), s32[]{:S(2)}) async-start(), calls=%async_computation.8 | async-start | bytes 131072 | tf_op jit(solution)/shard_map/psum | solution.py:290
  609.0 182.5 %all-reduce.7.cloned.1.call-start = ((), (), s32[]{:S(2)}) async-start(), calls=%async_computation.14 | async-start | bytes 5898240 | tf_op jit(solution)/shard_map/psum | solution.py:332
  618.7 11.6 %copy-start.42 = (f32[6,1]{0,1:T(1,128)S(1)}, f32[6,1]{0,1:T(1,128)}, u32[]{:S(2)}) copy-start(f32[6,1]{0,1:T(1,128)} %get-tuple-element.17) | copy-start | bytes 76
  618.7 172.8 %copy-start.7 = (bf16[288,576]{1,0:T(8,128)(2,1)S(1)}, bf16[288,576]{1,0:T(8,128)(2,1)}, u32[]{:S(2)}) copy-start(bf16[288,576]{1,0:T(8,128)(2,1)} %param.16) | copy-start | bytes 995332
  618.7 195.4 %copy-start.38 = (f32[288]{0:T(512)S(1)}, f32[288]{0:T(512)}, u32[]{:S(2)}) copy-start(f32[288]{0:T(512)} %copy-done.37) | copy-start | bytes 3460
  618.7 195.4 %copy-start.39 = (f32[288]{0:T(512)S(1)}, f32[288]{0:T(512)}, u32[]{:S(2)}) copy-start(f32[288]{0:T(512)} %get-tuple-element.44) | copy-start | bytes 3460
  (34 other events, 100.6 us)
Sparse Core Ops, SparseCore 0:
  10.2 60.8 all-gather.20
  73.2 56.5 all-gather.18
  131.4 22.6 all-gather.12
  155.5 24.0 all-gather.10
  181.0 37.4 all-gather.14
  219.9 37.4 all-gather.16
  267.7 79.4 reduce-scatter.11
  350.8 79.0 reduce-scatter.9
  519.1 55.2 all-gather.22
  605.2 24.2 reduce-scatter.7
  632.4 31.5 all-reduce.4
  667.5 123.9 all-reduce.6
where the time goes:
time: 829 us; the launch traced here: 824 us
  waiting for transfers between devices  514 us (62%)
  blocking collectives  125 us (15%)
  matrix products  69.4 us (8%)
  local copies, waits for them, and re-layouts  68.9 us (8%)
  other arithmetic  30.4 us (4%)
  between operations  15.1 us (2%)
    unnamed x14, waiting for transfers between devices  144 us
    psum x1, waiting for transfers between devices, body(): lax.psum(input_terms.astype(jnp.bfloat16), 'tensor').astype(jnp.float32)  126 us
    all_gather x2, waiting for transfers between devices, normalize(): whole_rows = lax.all_gather(hidden, 'tensor', axis=1, tiled=True)  87.5 us
    all_gather x1, waiting for transfers between devices, body(): lax.all_gather(grad_summed.astype(jnp.bfloat16), 'tensor', axis=1, tiled=...  55.1 us
    psum x1, blocking collectives, body(): scores = lax.psum(placed, ('dp', 'tensor'))  36.8 us
    all_gather x1, waiting for transfers between devices, body(): lax.all_gather(w_query, 'dp', axis=0, tiled=True)  32.4 us
    convert_element_type x4, local copies, waits for them, and re-layouts, normalize(): wide_rows = whole_rows.astype(jnp.float32)  25.6 us
    unnamed x98, local copies, waits for them, and re-layouts  24.7 us
  transfers between devices with their start and end apart: 12, of which 12 were waited for; matrix products, arithmetic and copies ran while one was open for 13% of the time, Pallas kernels for 0%

commit v1 on v0

--- a/solution.py
+++ b/solution.py
@@ -92,7 +92,9 @@
 
 
 def normalize(hidden, pre_gain):
-    whole_rows = lax.all_gather(hidden, "tensor", axis=1, tiled=True)
+    whole_rows = jnp.concatenate(
+        lax.all_to_all(jnp.stack([hidden] * lax.axis_size("tensor")), "tensor", 0, 0), axis=1
+    )
     wide_rows = whole_rows.astype(jnp.float32)
     pre_scale = lax.rsqrt(
         jnp.sum(wide_rows * wide_rows, axis=1, keepdims=True) / pre_gain.shape[0] + NORM_EPS

time: 829 us -> 827 us (level)
  waiting for transfers between devices: 514 us -> 388 us
  blocking collectives: 125 us -> 203 us
  local copies, waits for them, and re-layouts: 68.9 us -> 97.8 us
  other arithmetic: 30.4 us -> 39.8 us
    all_gather x2 -> x0, waiting for transfers between devices: 87.5 us -> none  [normalize(): whole_rows = lax.all_gather(hidden, 'tensor', axis=1, tiled=True)]
    all_to_all x0 -> x1, blocking collectives: none -> 74.4 us  [normalize(): lax.all_to_all(jnp.stack([hidden] * lax.axis_size('tensor')), 'tensor', 0...]
    all_gather x1, waiting for transfers between devices: 32.4 us -> 0.02 us  [body(): lax.all_gather(w_query, 'dp', axis=0, tiled=True)]
    all_to_all x0 -> x1, waiting for transfers between devices: none -> 31 us  [normalize(): lax.all_to_all(jnp.stack([hidden] * lax.axis_size('tensor')), 'tensor', 0...]
    all_gather x1, waiting for transfers between devices: 18.4 us -> 0.01 us  [body(): lax.all_gather(w_out, 'dp', axis=0, tiled=True)]
    all_gather x1, waiting for transfers between devices: 17.6 us -> 0.01 us  [body(): lax.all_gather(value_projection, 'dp', axis=0, tiled=True)]
    dot_general x0 -> x3, local copies, waits for them, and re-layouts: none -> 15.5 us  [the longest x1 6.74 us: attention_layer(): query_rows = jnp.dot(normed, w_query, preferred_element_type=jnp.float32)]
    convert_element_type x0 -> x3, local copies, waits for them, and re-layouts: none -> 14.4 us  [normalize(): normed = (wide_rows * pre_scale * pre_gain).astype(jnp.bfloat16)]
  transfers between devices with their start and end apart: 12 -> 11, of which waited for: 12 -> 7; matrix products, arithmetic and copies ran while one was open for 13% -> 16% of each run, Pallas kernels for 0% -> 0%
where the time goes in v1:
time: 827 us; the launch traced here: 815 us
  waiting for transfers between devices  388 us (47%)
  blocking collectives  203 us (25%)
  local copies, waits for them, and re-layouts  97.8 us (12%)
  matrix products  67.4 us (8%)
  other arithmetic  39.8 us (5%)
  between operations  15 us (2%)
    unnamed x12, waiting for transfers between devices  143 us
    psum x1, waiting for transfers between devices, body(): lax.psum(input_terms.astype(jnp.bfloat16), 'tensor').astype(jnp.float32)  126 us
    all_to_all x1, blocking collectives, normalize(): lax.all_to_all(jnp.stack([hidden] * lax.axis_size('tensor')), 'tensor', 0...  74.4 us
    all_gather x1, waiting for transfers between devices, body(): lax.all_gather(grad_summed.astype(jnp.bfloat16), 'tensor', axis=1, tiled=...  55.6 us
    psum x1, blocking collectives, body(): scores = lax.psum(placed, ('dp', 'tensor'))  37 us
    all_to_all x1, waiting for transfers between devices, normalize(): lax.all_to_all(jnp.stack([hidden] * lax.axis_size('tensor')), 'tensor', 0...  31 us
    unnamed x90, local copies, waits for them, and re-layouts  24.2 us
    psum x1, waiting for transfers between devices, body(): lax.psum(query_adapter_term.astype(jnp.bfloat16), 'dp').astype(jnp.float32)  22.5 us
  transfers between devices with their start and end apart: 11, of which 7 were waited for; matrix products, arithmetic and copies ran while one was open for 16% of the time, Pallas kernels for 0%

profile of v1, /device:TPU:0, one launch (start us, length us, event | category | flops | bytes accessed | tf_op | source)
XLA Modules:
  0.0 815.0 jit_solution(5075740816694369988)
XLA Ops:
  10.6 74.4 %all_to_all.10 = bf16[8,288,576]{2,1,0:T(8,128)(2,1)} all-to-all(bf16[8,288,576]{2,1,0:T(8,128)(2,1)S(1)} %stack.13), channel_id=1, replica_groups=mesh['dp'=4,'tensor'=8] {'tensor'}, dimensions={0} | all-to-all | bytes 5308416 | tf_op jit(solution)/shard_map/all_to_all | solution.py:96
  91.4 11.4 %all_gather.22 = bf16[4608,64]{0,1:T(8,128)(2,1)S(1)} all-gather(bf16[1152,64]{0,1:T(8,128)(2,1)} %param.26), channel_id=1, replica_groups=mesh['dp'=4,'tensor'=8] {'dp'}, dimensions={0}, use_global_device_ids=true | all-gather | bytes 737280 | tf_op jit(solution)/shard_map/all_gather | solution.py:196
  102.8 7.8 all_gather.23
  125.4 31.0 %all-to-all-done = bf16[8,288,576]{2,1,0:T(8,128)(2,1)S(1)} async-done(((bf16[8,288,576]{2,1,0:T(8,128)(2,1)}), bf16[8,288,576]{2,1,0:T(8,128)(2,1)S(1)}, u32[]{:S(2)}, u32[]{:S(2)}) %all-to-all-start) | async-done | bytes 2654240 | tf_op jit(solution)/shard_map/all_to_all | solution.py:96
  164.2 5.6 reshape.358
  170.2 5.9 copy.71
  176.1 7.3 reshape.351
  186.0 6.2 reshape.354
  202.7 6.7 copy.81
  231.7 5.5 convolution_convert_fusion
  248.7 5.6 convolution_convert_fusion.1
  261.1 59.4 %reduce-scatter.12.cloned.1.call-done = bf16[576,288]{1,0:T(8,128)(2,1)} async-done(((bf16[4608,288]{1,0:T(8,128)(2,1)}), bf16[576,288]{1,0:T(8,128)(2,1)}) %reduce-scatter.12.cloned.1.call-update) | async-done | bytes 331792
  322.5 80.6 %reduce-scatter.10.cloned.1.call-done = bf16[576,288]{1,0:T(8,128)(2,1)} async-done(((bf16[4608,288]{1,0:T(8,128)(2,1)}), bf16[576,288]{1,0:T(8,128)(2,1)}) %reduce-scatter.10.cloned.1.call-update) | async-done | bytes 331792
  406.8 20.7 %all-reduce = (f32[288]{0:T(512)}, f32[288]{0:T(512)}) all-reduce(f32[288]{0:T(512)} %fusion.69, f32[288]{0:T(512)} %fusion.56), channel_id=1, replica_groups=mesh['dp'=4,'tensor'=8] {'tensor'}, use_global_device_ids=true, to_apply=%region_4.5 | all-reduce | flops 576 | bytes 4608 | tf_op jit(solution)/shard_map/psum | solution.py:148
  439.7 37.0 %psum.65 = f32[2,12]{1,0:T(2,128)} all-reduce(f32[2,12]{1,0:T(2,128)} %dynamic_update_slice.3), channel_id=1, replica_groups=mesh['dp'=4,'tensor'=8] {'dp','tensor'}, use_global_device_ids=true, to_apply=%region_14.15 | all-reduce | flops 24 | bytes 192 | tf_op jit(solution)/shard_map/psum | solution.py:228
  486.8 21.8 %psum.66 = f32[288]{0:T(512)} all-reduce(f32[288]{0:T(512)} %fusion.62), channel_id=1, replica_groups=mesh['dp'=4,'tensor'=8] {'tensor'}, use_global_device_ids=true, to_apply=%region_17.18 | all-reduce | flops 288 | bytes 2304 | tf_op jit(solution)/shard_map/psum | solution.py:250
  510.8 55.6 %all-gather.15.cloned.1.call-done = bf16[8,576,288]{1,2,0:T(8,128)(2,1)} async-done(((bf16[1,576,288]{1,2,0:T(8,128)(2,1)}), bf16[8,576,288]{1,2,0:T(8,128)(2,1)}) %all-gather.15.cloned.1.call-update) | async-done | bytes 2654224 | tf_op jit(solution)/shard_map/all_gather | solution.py:255
  570.8 5.6 reshape.353
  576.4 5.4 convolution_convert_fusion.3
  611.4 9.6 %reduce-scatter.8.cloned.1.call-done = bf16[1152,128]{1,0:T(8,128)(2,1)} async-done(((bf16[4608,128]{1,0:T(8,128)(2,1)}), bf16[1152,128]{1,0:T(8,128)(2,1)}) %reduce-scatter.8.cloned.1.call-update) | async-done | bytes 294928 | tf_op jit(solution)/shard_map/reduce_scatter | solution.py:317
  622.0 10.3 %psum.71 = bf16[64,256]{1,0:T(8,128)(2,1)S(1)} all-reduce(bf16[64,256]{1,0:T(8,128)(2,1)S(1)} %fusion.47), channel_id=1, replica_groups=mesh['dp'=4,'tensor'=8] {'dp'}, use_global_device_ids=true, to_apply=%region_25.26 | all-reduce | flops 16384 | bytes 65536 | tf_op jit(solution)/shard_map/psum | solution.py:293
  632.9 22.5 %all-reduce.5.cloned.1.call-done = bf16[64,512]{1,0:T(8,128)(2,1)} async-done(((bf16[64,512]{1,0:T(8,128)(2,1)}), bf16[64,512]{1,0:T(8,128)(2,1)}) %all-reduce.5.cloned.1.call-update) | async-done | bytes 65552 | tf_op jit(solution)/shard_map/psum | solution.py:292
  657.0 126.0 %all-reduce.7.cloned.1.call-done = (bf16[288,4608]{1,0:T(8,128)(2,1)}, bf16[1152,128]{1,0:T(8,128)(2,1)}) async-done(((bf16[288,4608]{1,0:T(8,128)(2,1)}, bf16[1152,128]{1,0:T(8,128)(2,1)}), (bf16[288,4608]{1,0:T(8,128)(2,1)}, bf16[1152,128]{1,0:T(8,128)(2,1)})) %all-reduce.7.cloned.1.call-update) | async-done | bytes 2949136 | tf_op jit(solution)/shard_map/psum | solution.py:334
  784.3 19.4 %psum.68 = f32[288]{0:T(512)S(1)} all-reduce(f32[288]{0:T(512)S(1)} %fusion.59), channel_id=1, replica_groups=mesh['dp'=4,'tensor'=8] {'tensor'}, use_global_device_ids=true, to_apply=%region_21.22 | all-reduce | flops 288 | bytes 2304 | tf_op jit(solution)/shard_map/psum | solution.py:337
  (208 shorter events, 158.3 us)
Async XLA Ops:
  7.2 206.1 %copy-start = (bf16[64,512]{1,0:T(8,128)(2,1)S(1)}, bf16[64,512]{1,0:T(8,128)(2,1)}, u32[]{:S(2)}) copy-start(bf16[64,512]{1,0:T(8,128)(2,1)} %param.28) | copy-start | bytes 196612
  7.2 106.8 %all-gather.7.cloned.1.call-start = ((), (), s32[]{:S(2)}) async-start(), calls=%async_computation.5 | async-start | bytes 2949120 | tf_op jit(solution)/shard_map/all_gather | solution.py:194
  7.9 110.5 %all-gather.9.cloned.1.call-start = ((), (), s32[]{:S(2)}) async-start(), calls=%async_computation.6 | async-start | bytes 2949120 | tf_op jit(solution)/shard_map/all_gather | solution.py:193
  8.7 194.0 %all-gather.11.cloned.1.call-start = ((), (), s32[]{:S(2)}) async-start(), calls=%async_computation.7 | async-start | bytes 5898240 | tf_op jit(solution)/shard_map/all_gather | solution.py:192
  10.6 74.4 %copy-start.5 = (bf16[288,576]{1,0:T(8,128)(2,1)S(1)}, bf16[288,576]{1,0:T(8,128)(2,1)}, u32[]{:S(2)}) copy-start(bf16[288,576]{1,0:T(8,128)(2,1)} %param.16) | copy-start | bytes 995332
  86.9 69.5 %all-to-all-start = ((bf16[8,288,576]{2,1,0:T(8,128)(2,1)}), bf16[8,288,576]{2,1,0:T(8,128)(2,1)S(1)}, u32[]{:S(2)}, u32[]{:S(2)}) async-start(bf16[8,288,576]{2,1,0:T(8,128)(2,1)} %stack.12), calls=%async_computation | async-start | bytes 5898240 | tf_op jit(solution)/shard_map/all_to_all | solution.py:96
  90.7 20.0 %copy-start.36 = (s32[3]{0:T(128)S(1)}, s32[3]{0:T(128)}, u32[]{:S(2)}) copy-start(s32[3]{0:T(128)} %param.18) | copy-start | bytes 40
  90.7 141.0 %all-gather.13.cloned.1.call-start = ((), (), s32[]{:S(2)}) async-start(), calls=%async_computation.8 | async-start | bytes 5898240 | tf_op jit(solution)/shard_map/all_gather | solution.py:195
  91.2 229.3 %reduce-scatter.12.cloned.1.call-start = ((), (), s32[]{:S(2)}) async-start(), calls=%async_computation.13 | async-start | bytes 3981312
  112.3 84.0 %copy-start.15 = (f32[96,64]{1,0:T(8,128)}, f32[96,64]{1,0:T(8,128)S(1)}, u32[]{:S(2)}) copy-start(f32[96,64]{1,0:T(8,128)S(1)} %get-tuple-element.45) | copy-start | bytes 73732
  112.3 110.1 %copy-start.12 = (f32[96,64]{1,0:T(8,128)}, f32[96,64]{1,0:T(8,128)S(1)}, u32[]{:S(2)}) copy-start(f32[96,64]{1,0:T(8,128)S(1)} %get-tuple-element.46) | copy-start | bytes 73732
  157.7 39.7 %copy-start.32 = (f32[288]{0:T(512)}, f32[288]{0:T(512)S(1)}, u32[]{:S(2)}) copy-start(f32[288]{0:T(512)S(1)} %get-tuple-element.41) | copy-start | bytes 3460
  241.9 161.2 %reduce-scatter.10.cloned.1.call-start = ((), (), s32[]{:S(2)}) async-start(), calls=%async_computation.12 | async-start | bytes 3981312
  259.0 307.3 %all-gather.15.cloned.1.call-start = ((), (), s32[]{:S(2)}) async-start(), calls=%async_computation.11 | async-start | bytes 3317760 | tf_op jit(solution)/shard_map/all_gather | solution.py:255
  510.7 110.3 %reduce-scatter.8.cloned.1.call-start = ((), (), s32[]{:S(2)}) async-start(), calls=%async_computation.9 | async-start | bytes 1474560 | tf_op jit(solution)/shard_map/reduce_scatter | solution.py:317
  576.4 8.5 %copy-start.28 = (pred[3,96,96]{1,2,0:T(8,128)(4,1)S(1)}, pred[3,96,96]{1,2,0:T(8,128)(4,1)}, u32[]{:S(2)}) copy-start(pred[3,96,96]{1,2,0:T(8,128)(4,1)} %broadcast_and_fusion) | copy-start | bytes 82948
  576.4 8.5 %copy-start.41 = (f32[3,2,2,96]{3,2,1,0:T(2,128)S(1)}, f32[3,2,2,96]{3,2,1,0:T(2,128)}, u32[]{:S(2)}) copy-start(f32[3,2,2,96]{3,2,1,0:T(2,128)} %copy-done.40) | copy-start | bytes 13828
  596.6 58.9 %all-reduce.5.cloned.1.call-start = ((), (), s32[]{:S(2)}) async-start(), calls=%async_computation.10 | async-start | bytes 131072 | tf_op jit(solution)/shard_map/psum | solution.py:292
  600.4 182.5 %all-reduce.7.cloned.1.call-start = ((), (), s32[]{:S(2)}) async-start(), calls=%async_computation.14 | async-start | bytes 5898240 | tf_op jit(solution)/shard_map/psum | solution.py:334
  611.3 9.8 %copy-start.38 = (f32[6,1]{0,1:T(1,128)S(1)}, f32[6,1]{0,1:T(1,128)}, u32[]{:S(2)}) copy-start(f32[6,1]{0,1:T(1,128)} %get-tuple-element.17) | copy-start | bytes 76
  611.3 194.2 %copy-start.6 = (bf16[288,576]{1,0:T(8,128)(2,1)S(1)}, bf16[288,576]{1,0:T(8,128)(2,1)}, u32[]{:S(2)}) copy-start(bf16[288,576]{1,0:T(8,128)(2,1)} %param.17) | copy-start | bytes 995332
  611.3 194.2 %copy-start.29 = (f32[288]{0:T(512)S(1)}, f32[288]{0:T(512)}, u32[]{:S(2)}) copy-start(f32[288]{0:T(512)} %mul.780) | copy-start | bytes 3460
  611.3 194.2 %copy-start.33 = (f32[288]{0:T(512)S(1)}, f32[288]{0:T(512)}, u32[]{:S(2)}) copy-start(f32[288]{0:T(512)} %copy-done.32) | copy-start | bytes 3460
  611.3 194.2 %copy-start.35 = (f32[288]{0:T(512)S(1)}, f32[288]{0:T(512)}, u32[]{:S(2)}) copy-start(f32[288]{0:T(512)} %get-tuple-element.40) | copy-start | bytes 3460
  (29 other events, 73.1 us)
Sparse Core Ops, SparseCore 0:
  9.5 26.7 all-gather.6
  37.9 24.0 all-gather.8
  63.6 40.5 all-gather.10
  105.6 37.4 all-gather.12
  242.0 78.5 reduce-scatter.11
  324.0 79.0 reduce-scatter.9
  510.8 55.4 all-gather.14
  596.7 24.2 reduce-scatter.7
  623.9 31.5 all-reduce.4
  659.0 123.9 all-reduce.6
